TPU v7x, 32 devices: a whole 2x2x4 slice. The times are simulated.
32 devices in a mesh: cp: 16 (over z, x, core), tp: 2 (over y).
Axes of the slice: x: 2, y: 2, z: 4, core: 2. Of those that a mesh axis runs over, the one named last changes fastest.
Arguments:
- hidden: bfloat16 [8192, 4096], P('cp', 'tp'), may hold values from -6 to 6
- norm_gain: float32 [4096], replicated, may hold values from 0.5 to 1.5
- w_query: bfloat16 [4096, 4096], P(None, 'tp'), may hold values from -0.140625 to 0.140625
- w_key: bfloat16 [4096, 1024], P(None, 'tp'), may hold values from -4 to 4
- w_value: bfloat16 [4096, 1024], P(None, 'tp'), may hold values from -0.09375 to 0.09375
- w_out: bfloat16 [4096, 4096], P('tp'), may hold values from -0.5 to 0.5
- doc_ids: int32 [8192], P('cp'), may hold values from 0 to 5, never falling along the last dimension, each value on 1 to 6144 neighbouring positions
Outputs:
- updated: bfloat16 [8192, 4096], P('cp', 'tp')
Inputs may be any that keep to these rules, and one draw needn't show every extreme that they name: `doc_ids`: document numbers never fall along the sequence; every document has 1 to 6144 tokens.
All inputs are finite; a program needn't handle non-finite values.
Results may differ from a plain program's by a relative error of at most 0.017.
The roundings to bfloat16 on the way count: a program that leaves them out, or rounds other values in their place, can miss the bound.
Values may be sent and summed in bfloat16 or wider, within the bound.
A program may use at most 128 MiB of HBM per device.

v0:
```python
import functools

import jax
import jax.numpy as jnp
from jax import lax
from jax.experimental import pallas as pl
from jax.experimental.pallas import tpu as pltpu
from jax.sharding import PartitionSpec as P

HEADS = 32
KV_HEADS = 8
HEAD_SIZE = 128
GROUP = HEADS // KV_HEADS

epsilon = 1e-05
rope_base = 500000.0
LOG2E = 1.4426950408889634
SCALE = HEAD_SIZE ** (-0.5) * LOG2E
FLOOR = -1e29
MASKED = -1e30
CHUNK = 128
QTILE = 128
NEAR = 8
LANES = 128
MESH = pl.DeviceIdType.MESH


def tables(positions):
    half = HEAD_SIZE // 2
    freqs = rope_base ** (-jnp.arange(half, dtype=jnp.float32) * 2.0 / HEAD_SIZE)
    angles = positions.astype(jnp.float32)[:, None] * freqs[None, :]
    cosine = jnp.cos(angles)
    sine = jnp.sin(angles)
    return (
        jnp.concatenate([cosine, cosine], axis=1),
        jnp.concatenate([-sine, sine], axis=1),
    )


def columns_of(n_cp):
    chips = n_cp // 2
    cols = 1
    while cols * cols * 4 <= chips:
        cols *= 2
    return cols


def layer_kernel(
    hid_hbm, gain_ref, wq_hbm, wk_hbm, wv_hbm, wo_hbm, cos_ref, sin_ref, docs_ref, qdoc_ref,
    out_hbm,
    hid, wq, wkv, kv, q, normed, acc, ml, docs, recv, stage,
    hid_send, hid_recv, own_sem, w_sem, doc_send, doc_recv, kv_send, kv_recv,
    part_send, part_recv, out_sem,
    *, n_cp, n_tp, longest,
):
    tok, feat = hid_hbm.shape
    width = gain_ref.shape[1]
    q_cols = wq.shape[1]
    kv_cols = wkv.shape[1]
    n_kv = kv_cols // (2 * HEAD_SIZE)
    chunks = tok // CHUNK
    n_tiles = tok // QTILE
    cols = columns_of(n_cp)
    rows_z = n_cp // (2 * cols)
    window = min((longest + tok - 2) // tok, n_cp - 1)
    chip_window = (window + 1) // 2
    near = min(NEAR, window + 1)

    me = lax.axis_index("cp")
    rank = lax.axis_index("tp")
    core = lax.rem(me, 2)
    my_x = lax.rem(me // 2, cols)
    my_z = me // (2 * cols)

    def peer_of(by):
        return lax.rem(rank + by, n_tp)

    barrier = pltpu.get_barrier_semaphore()
    for by in range(1, n_tp):
        pl.semaphore_signal(barrier, inc=1, device_id={"tp": peer_of(by)}, device_id_type=MESH)

    def greet(by, carry):
        pl.semaphore_signal(
            barrier, inc=1, device_id={"cp": lax.rem(me + by, n_cp)}, device_id_type=MESH
        )
        return carry

    lax.fori_loop(1, n_cp, greet, 0)

    wk_copy = pltpu.make_async_copy(wk_hbm, wkv.at[:, pl.ds(0, kv_cols // 2)], w_sem.at[0])
    wv_copy = pltpu.make_async_copy(
        wv_hbm, wkv.at[:, pl.ds(kv_cols // 2, kv_cols // 2)], w_sem.at[1]
    )
    wq_copy = pltpu.make_async_copy(wq_hbm, wq, w_sem.at[2])
    own_copy = pltpu.make_async_copy(hid_hbm, hid.at[rank], own_sem)
    own_copy.start()
    wk_copy.start()
    wv_copy.start()
    wq_copy.start()
    docs[me] = docs_ref[...]
    pl.semaphore_wait(barrier, n_cp - 1 + n_tp - 1)

    def hid_copy(by, t):
        rows = pl.ds(t * CHUNK, CHUNK)
        return pltpu.make_async_remote_copy(
            src_ref=hid_hbm.at[rows],
            dst_ref=hid.at[rank, rows],
            send_sem=hid_send.at[by - 1, t],
            recv_sem=hid_recv.at[n_tp - 1 - by, t],
            device_id={"tp": peer_of(by)},
            device_id_type=MESH,
        )

    for t in range(chunks):
        for by in range(1, n_tp):
            hid_copy(by, t).start()

    def doc_copy(source, target):
        return pltpu.make_async_remote_copy(
            src_ref=docs_ref,
            dst_ref=docs.at[source],
            send_sem=doc_send.at[target],
            recv_sem=doc_recv.at[source],
            device_id={"cp": target},
            device_id_type=MESH,
        )

    last_target = jnp.minimum(me + window, n_cp - 1)

    def doc_start(target, carry):
        doc_copy(me, target).start()
        return carry

    lax.fori_loop(me + 1, last_target + 1, doc_start, 0)

    def takes(z, x, zs, xs):
        reach = z * cols - (zs * cols + xs) <= chip_window
        by_z = (xs == x) & (zs < z) & reach
        from_left = (xs < x) & (zs <= z) & (z * cols + x - (zs * cols + xs) <= chip_window)
        from_right = (xs > x) & (zs < z) & reach
        return by_z | from_left | from_right

    def block_copy(direction, zs, xs, ks, t, target):
        chip = zs * cols + xs
        s = chip * 2 + ks
        rows = pl.ds(pl.multiple_of(s * tok + t * CHUNK, CHUNK), CHUNK)
        return pltpu.make_async_remote_copy(
            src_ref=kv.at[rows],
            dst_ref=kv.at[rows],
            send_sem=kv_send.at[direction, chip * chunks + t],
            recv_sem=kv_recv.at[s * chunks + t],
            device_id={"cp": target},
            device_id_type=MESH,
        )

    def hops(zs, xs):
        own_chip = (zs == my_z) & (xs == my_x)
        return (
            ((xs == my_x) & (my_z + 1 < rows_z) & takes(my_z + 1, my_x, zs, xs), me + 2 * cols),
            ((xs <= my_x) & (my_x + 1 < cols) & takes(my_z, my_x + 1, zs, xs), me + 2),
            ((xs >= my_x) & (my_x >= 1) & takes(my_z, my_x - 1, zs, xs), me - 2),
            (jnp.logical_not(own_chip) | (core == 0), me + 1 - 2 * core),
        )

    def forward(zs, xs, t):
        for direction, (wanted, target) in enumerate(hops(zs, xs)):
            @pl.when(wanted)
            def _():
                block_copy(direction, zs, xs, core, t, target).start()

    def arrive(zs, xs, ks, t, relay):
        in_range = (zs >= 0) & (xs >= 0) & (xs < cols) & (t >= 0) & (t < chunks)
        own_chip = (zs == my_z) & (xs == my_x)
        if relay:
            wanted = in_range & takes(my_z, my_x, zs, xs)
        else:
            wanted = in_range & (takes(my_z, my_x, zs, xs) | (own_chip & (core == 1)))

        @pl.when(wanted)
        def _():
            block_copy(0, zs, xs, ks, t, me).wait_recv()
            if relay:
                forward(zs, xs, t)

    def handle_round(r):
        def along_z(dz, carry):
            arrive(my_z - dz, my_x, core, r - dz, True)
            return carry

        lax.fori_loop(1, rows_z, along_z, 0)
        for dx in range(1, cols):
            def along_x(dz, carry):
                arrive(my_z - dz, my_x - dx, core, r - dz, True)
                arrive(my_z - dz, my_x + dx, core, r - dz, True)
                return carry

            lax.fori_loop(0, rows_z, along_x, 0)

        def along_core(i, carry):
            arrive(my_z - i // cols, lax.rem(i, cols), 1 - core, r - i // cols, False)
            return carry

        lax.fori_loop(0, rows_z * cols, along_core, 0)

    own_copy.wait()
    wk_copy.wait()
    wv_copy.wait()
    part_rows = 32

    def rope(raw, cosine, sine):
        turned = raw * cosine + pltpu.roll(raw, HEAD_SIZE // 2, 1) * sine
        return turned.astype(jnp.bfloat16)

    def chunk_step(t, carry):
        base = pl.multiple_of(t * CHUNK, CHUNK)
        for by in range(1, n_tp):
            pltpu.make_async_remote_copy(
                src_ref=hid.at[peer_of(by), pl.ds(base, CHUNK)],
                dst_ref=hid.at[peer_of(by), pl.ds(base, CHUNK)],
                send_sem=hid_send.at[by - 1, t],
                recv_sem=hid_recv.at[by - 1, t],
                device_id={"tp": peer_of(by)},
                device_id_type=MESH,
            ).wait_recv()

        def norm_part(i, carry):
            rows = pl.ds(pl.multiple_of(base + i * part_rows, part_rows), part_rows)
            total = jnp.zeros((part_rows, LANES), jnp.float32)
            for j in range(n_tp):
                wide = hid[j, rows, :].astype(jnp.float32)
                square = wide * wide
                for c in range(feat // LANES):
                    total = total + square[:, c * LANES : (c + 1) * LANES]
            mean = jnp.sum(total, axis=1, keepdims=True) / width
            inverse_rms = lax.rsqrt(mean + epsilon)
            out_rows = pl.ds(pl.multiple_of(i * part_rows, part_rows), part_rows)
            for j in range(n_tp):
                wide = hid[j, rows, :].astype(jnp.float32)
                gain = gain_ref[:, j * feat : (j + 1) * feat]
                normed[out_rows, j * feat : (j + 1) * feat] = (
                    wide * inverse_rms * gain
                ).astype(jnp.bfloat16)
            return carry

        lax.fori_loop(0, CHUNK // part_rows, norm_part, 0)
        rows = pl.ds(base, CHUNK)
        cosine = cos_ref[rows, :]
        sine = sin_ref[rows, :]
        own_rows = pl.ds(pl.multiple_of(me * tok + t * CHUNK, CHUNK), CHUNK)
        for g in range(2 * n_kv):
            lanes = slice(g * HEAD_SIZE, (g + 1) * HEAD_SIZE)
            if g % 2 == 0:
                pair = jnp.dot(
                    normed[...],
                    wkv[:, g * HEAD_SIZE : (g + 2) * HEAD_SIZE],
                    preferred_element_type=jnp.float32,
                )
            raw = pair[:, (g % 2) * HEAD_SIZE : (g % 2 + 1) * HEAD_SIZE]
            kv[own_rows, lanes] = rope(raw, cosine, sine) if g < n_kv else raw.astype(jnp.bfloat16)

        @pl.when(t == 0)
        def _():
            wq_copy.wait()

        def query_group(g, carry):
            cut = pl.multiple_of(g * GROUP * HEAD_SIZE, HEAD_SIZE)
            raw = jnp.dot(
                normed[...],
                wq[:, pl.ds(cut, GROUP * HEAD_SIZE)],
                preferred_element_type=jnp.float32,
            )
            for h in range(GROUP):
                q[g * GROUP + h, rows, :] = rope(
                    raw[:, h * HEAD_SIZE : (h + 1) * HEAD_SIZE], cosine, sine
                )
            return carry

        query_group(0, 0)
        forward(my_z, my_x, t)
        lax.fori_loop(1, n_kv, query_group, 0)
        handle_round(t - 1)
        return carry

    lax.fori_loop(0, chunks, chunk_step, 0)

    wo_copies = [
        pltpu.make_async_copy(
            wo_hbm.at[:, pl.ds(j * feat, feat)], wq.at[pl.ds(j * q_cols, q_cols)], w_sem.at[3 + j]
        )
        for j in range(n_tp)
    ]
    for copy in wo_copies:
        copy.start()

    strips = feat // LANES
    block_lanes = tok // LANES
    lane = lax.broadcasted_iota(jnp.int32, (QTILE, LANES), 1)
    low_half = lane < LANES // 2

    def doc_strip(s):
        return s // strips, pl.ds(pl.multiple_of(lax.rem(s, strips) * LANES, LANES), LANES)

    def key_docs(s):
        row = jnp.broadcast_to(docs[s], (LANES, tok))
        number = lax.broadcasted_iota(jnp.int32, (LANES, tok), 0)
        one_hot = jnp.where(row == number, 1.0, 0.0).astype(jnp.float32)
        j, lanes = doc_strip(s)
        hid[j, :, lanes] = one_hot.T.astype(jnp.bfloat16)

    def attend(g, tile, s, first):
        key_rows = pl.ds(pl.multiple_of(s * tok, tok), tok)
        j, lanes = doc_strip(s)
        key_lanes = pl.ds(pl.multiple_of(g * HEAD_SIZE, HEAD_SIZE), HEAD_SIZE)
        value_lanes = pl.ds(pl.multiple_of((n_kv + g) * HEAD_SIZE, HEAD_SIZE), HEAD_SIZE)
        keys = jnp.concatenate([kv[key_rows, key_lanes], hid[j, :, lanes]], axis=1)
        values = jnp.concatenate(
            [kv[key_rows, value_lanes], jnp.ones((tok, LANES), jnp.bfloat16)], axis=1
        )
        rows = pl.ds(pl.multiple_of(tile * QTILE, QTILE), QTILE)
        if first:
            row = lax.broadcasted_iota(jnp.int32, (QTILE, LANES), 0) + tile * QTILE
        for h in range(GROUP):
            head = g * GROUP + h
            queries = jnp.concatenate([q[head, rows, :], qdoc_ref[rows, :]], axis=1)
            scores = lax.dot_general(
                queries, keys, (((1,), (1,)), ((), ())), preferred_element_type=jnp.float32
            )
            pieces = [
                scores[:, c * LANES : (c + 1) * LANES] * SCALE for c in range(block_lanes)
            ]
            if first:
                pieces = [
                    jnp.where(row >= lane + c * LANES, p, MASKED) for c, p in enumerate(pieces)
                ]
            top = functools.reduce(jnp.maximum, pieces)
            top = jnp.max(top, axis=1, keepdims=True)
            if first:
                new = jnp.broadcast_to(jnp.maximum(top, FLOOR), (QTILE, LANES))
            else:
                packed = ml[head, rows, :]
                turned = pltpu.roll(packed, LANES // 2, 1)
                old = jnp.where(low_half, packed, turned)
                total = jnp.where(low_half, turned, packed)
                new = jnp.maximum(old, top)
                correction = jnp.exp2(old - new)
            weights = jnp.concatenate(
                [jnp.exp2(p - new).astype(jnp.bfloat16) for p in pieces], axis=1
            )
            sums = jnp.dot(weights, values, preferred_element_type=jnp.float32)
            if first:
                acc[head, rows, :] = sums[:, :HEAD_SIZE]
                ml[head, rows, :] = jnp.where(low_half, new, sums[:, HEAD_SIZE:])
            else:
                acc[head, rows, :] = acc[head, rows, :] * correction + sums[:, :HEAD_SIZE]
                ml[head, rows, :] = jnp.where(
                    low_half, new, total * correction + sums[:, HEAD_SIZE:]
                )

    def all_tiles(s, first):
        def one(i, carry):
            attend(i // n_tiles, lax.rem(i, n_tiles), s, first)
            return carry

        lax.fori_loop(0, n_kv * n_tiles, one, 0)

    key_docs(me)
    all_tiles(me, True)

    in_row = lax.rem(me, 2 * cols) + 1
    last_round = chunks - 1 + rows_z - 1

    def rounds_before(o):
        distance = jnp.where(o < in_row, 0, (o - in_row) // (2 * cols) + 1)
        return jnp.clip(
            jnp.maximum(chunks - 1 + o // 2, chunks - 1 + distance), chunks - 1, last_round
        )

    def take_rounds(begin, end):
        def one(r, carry):
            handle_round(r)
            return carry

        lax.fori_loop(begin, end, one, 0)

    def docs_for(s):
        doc_copy(s, me).wait_recv()
        key_docs(s)

    def near_step(o, carry):
        take_rounds(jnp.where(o == 1, chunks - 1, rounds_before(o - 1) + 1), rounds_before(o) + 1)
        s = me - o

        @pl.when(s >= 0)
        def _():
            docs_for(s)
            all_tiles(s, False)

        return carry

    lax.fori_loop(1, near, near_step, 0)
    take_rounds(rounds_before(near - 1) + 1, last_round + 1)

    def far_docs(o, carry):
        @pl.when(me - o >= 0)
        def _():
            docs_for(me - o)

        return carry

    lax.fori_loop(near, window + 1, far_docs, 0)
    for copy in wo_copies:
        copy.wait()

    far_end = jnp.minimum(window, me) + 1
    col_step = min(512, feat)

    def part_copy(by, tile):
        rows = pl.ds(pl.multiple_of(tile * QTILE, QTILE), QTILE)
        return pltpu.make_async_remote_copy(
            src_ref=stage.at[by - 1, rows],
            dst_ref=recv.at[n_tp - 1 - by, rows],
            send_sem=part_send.at[by - 1, tile],
            recv_sem=part_recv.at[n_tp - 1 - by, tile],
            device_id={"tp": peer_of(by)},
            device_id_type=MESH,
        )

    def tile_step(tile, carry):
        rows = pl.ds(pl.multiple_of(tile * QTILE, QTILE), QTILE)

        def far_step(i, carry):
            attend(lax.rem(i, n_kv), tile, me - near - i // n_kv, False)
            return carry

        lax.fori_loop(0, jnp.maximum(far_end - near, 0) * n_kv, far_step, 0)

        def finish(head, carry):
            packed = ml[head, rows, :]
            total = jnp.where(low_half, pltpu.roll(packed, LANES // 2, 1), packed)
            lanes = pl.ds(pl.multiple_of(head * HEAD_SIZE, HEAD_SIZE), HEAD_SIZE)
            normed[:, lanes] = (acc[head, rows, :] / total).astype(jnp.bfloat16)
            return carry

        lax.fori_loop(0, n_kv * GROUP, finish, 0)
        attended = normed[:, :q_cols]
        for by in list(range(1, n_tp)) + [0]:
            piece = pl.ds(pl.multiple_of(peer_of(by) * q_cols, q_cols), q_cols)
            for c in range(feat // col_step):
                part = jnp.dot(
                    attended,
                    wq[piece, c * col_step : (c + 1) * col_step],
                    preferred_element_type=jnp.float32,
                ).astype(jnp.bfloat16)
                if by:
                    stage[by - 1, rows, c * col_step : (c + 1) * col_step] = part
                else:
                    for h in range(col_step // LANES):
                        q[c * (col_step // LANES) + h, rows, :] = part[
                            :, h * LANES : (h + 1) * LANES
                        ]
        for by in range(1, n_tp):
            part_copy(by, tile).start()
        return carry

    lax.fori_loop(0, n_tiles, tile_step, 0)

    def out_copy(tile):
        rows = pl.ds(pl.multiple_of(tile * QTILE, QTILE), QTILE)
        return pltpu.make_async_copy(recv.at[0, rows], out_hbm.at[rows], out_sem.at[tile])

    def sum_step(tile, carry):
        rows = pl.ds(pl.multiple_of(tile * QTILE, QTILE), QTILE)
        for by in range(1, n_tp):
            part_copy(by, tile).wait_recv()
        for c in range(feat // LANES):
            lanes = slice(c * LANES, (c + 1) * LANES)
            total = q[c, rows, :].astype(jnp.float32)
            for by in range(1, n_tp):
                total = total + recv[by - 1, rows, lanes].astype(jnp.float32)
            recv[0, rows, lanes] = total.astype(jnp.bfloat16)
        out_copy(tile).start()
        return carry

    lax.fori_loop(0, n_tiles, sum_step, 0)

    def sent_step(i, carry):
        t = lax.rem(i, chunks)
        chip = i // chunks
        zs, xs = chip // cols, lax.rem(chip, cols)
        own_chip = (zs == my_z) & (xs == my_x)
        held = own_chip | ((zs <= my_z) & takes(my_z, my_x, zs, xs))
        for direction, (wanted, target) in enumerate(hops(zs, xs)):
            @pl.when(held & wanted)
            def _():
                block_copy(direction, zs, xs, core, t, target).wait_send()

        return carry

    lax.fori_loop(0, n_cp // 2 * chunks, sent_step, 0)

    def doc_sent(target, carry):
        doc_copy(me, target).wait_send()
        return carry

    lax.fori_loop(me + 1, last_target + 1, doc_sent, 0)
    for t in range(chunks):
        for by in range(1, n_tp):
            hid_copy(by, t).wait_send()

    def end_step(tile, carry):
        for by in range(1, n_tp):
            part_copy(by, tile).wait_send()
        out_copy(tile).wait()
        return carry

    lax.fori_loop(0, n_tiles, end_step, 0)


def shards(hidden, norm_gain, w_query, w_key, w_value, w_out, doc_ids, *, n_cp, n_tp):
    tok, feat = hidden.shape
    width = norm_gain.shape[0]
    q_cols = w_query.shape[1]
    kv_cols = 2 * w_key.shape[1]
    seq = tok * n_cp
    longest = seq * 3 // 4
    chunks = tok // CHUNK
    n_tiles = tok // QTILE
    cp_rank = lax.axis_index("cp")
    positions = cp_rank * tok + jnp.arange(tok, dtype=jnp.int32)
    cosine, sine = tables(positions)
    number = jnp.arange(LANES, dtype=jnp.int32)
    other_docs = jnp.where(doc_ids[:, None] == number[None, :], 0.0, MASKED).astype(jnp.bfloat16)
    vmem = pl.BlockSpec(memory_space=pltpu.VMEM)
    hbm = pl.BlockSpec(memory_space=pl.ANY)
    bf16, f32 = jnp.bfloat16, jnp.float32
    dma = pltpu.SemaphoreType.DMA
    heads = q_cols // HEAD_SIZE
    return pl.pallas_call(
        functools.partial(layer_kernel, n_cp=n_cp, n_tp=n_tp, longest=longest),
        out_shape=jax.ShapeDtypeStruct((tok, feat), bf16),
        in_specs=[hbm, vmem, hbm, hbm, hbm, hbm, vmem, vmem, vmem, vmem],
        out_specs=hbm,
        scratch_shapes=[
            pltpu.VMEM((n_tp, tok, feat), bf16),
            pltpu.VMEM((width, q_cols), bf16),
            pltpu.VMEM((width, kv_cols), bf16),
            pltpu.VMEM((seq, kv_cols), bf16),
            pltpu.VMEM((heads, tok, HEAD_SIZE), bf16),
            pltpu.VMEM((CHUNK, width), bf16),
            pltpu.VMEM((heads, tok, HEAD_SIZE), f32),
            pltpu.VMEM((heads, tok, LANES), f32),
            pltpu.VMEM((n_cp, 1, tok), jnp.int32),
            pltpu.VMEM((n_tp - 1, tok, feat), bf16),
            pltpu.VMEM((n_tp - 1, tok, feat), bf16),
            dma((n_tp - 1, chunks)),
            dma((n_tp - 1, chunks)),
            dma(()),
            dma((3 + n_tp,)),
            dma((n_cp,)),
            dma((n_cp,)),
            dma((4, n_cp // 2 * chunks)),
            dma((n_cp * chunks,)),
            dma((n_tp - 1, n_tiles)),
            dma((n_tp - 1, n_tiles)),
            dma((n_tiles,)),
        ],
        compiler_params=pltpu.CompilerParams(
            collective_id=0, has_side_effects=True, vmem_limit_bytes=67_000_000
        ),
    )(
        hidden, norm_gain[None, :], w_query, w_key, w_value, w_out, cosine, sine,
        doc_ids[None, :], other_docs,
    )


def solution(mesh):
    in_specs = (
        P("cp", "tp"),
        P(),
        P(None, "tp"),
        P(None, "tp"),
        P(None, "tp"),
        P("tp", None),
        P("cp"),
    )
    body = functools.partial(shards, n_cp=mesh.shape["cp"], n_tp=mesh.shape["tp"])
    return jax.shard_map(
        body, mesh=mesh, in_specs=in_specs, out_specs=P("cp", "tp"), check_vma=False
    )
```

profile of v0, /device:TPU:28, one launch (start us, length us, event | category | flops | bytes accessed | tf_op | source)
XLA Modules:
  0.0 501.1 jit_solution(4824937524193642113)
XLA Ops:
  0.0 1.5 select_convert_fusion.qdoc_ref
  1.5 1.0 fusion
  2.5 1.0 pad_maximum_fusion
  3.5 494.4 %shard_map.73 = bf16[512,2048]{1,0:T(8,128)(2,1)} custom-call(bf16[512,2048]{1,0:T(8,128)(2,1)} %hid_hbm.1, f32[1,4096]{1,0:T(1,128)} %bitcast.2, bf16[4096,2048]{1,0:T(8,128)(2,1)} %wq_hbm.1, bf16[4096,512]{1,0:T(8,128)(2,1)} %wk_hbm.1, bf16[4096,512]{1,0:T(8,128)(2,1)} %wv_hbm.1, bf16[2048,4096]{1,0:T(8,128)(2,1)} %wo_hbm.1, ...), custom_call_target="tpu_custom_call" | custom-call | tf_op jit(solution)/shard_map/pallas_call | solution.py:538
  497.9 3.2 copy.9
  (2 shorter events, 0.0 us)
where the time goes:
time: 501 us
  Pallas kernels  494 us (99%)
    pallas_call x1, Pallas kernels, shards(): pl.pallas_call(functools.partial(layer_kernel, n_cp=n_cp, n_tp=n_tp, long...  494 us

commit v1 on v0

v1 whole, which is shorter than its diff:
```python
import functools

import jax
import jax.numpy as jnp
from jax import lax
from jax.experimental import pallas as pl
from jax.experimental.pallas import tpu as pltpu
from jax.sharding import PartitionSpec as P

HEADS = 32
KV_HEADS = 8
HEAD_SIZE = 128
GROUP = HEADS // KV_HEADS

epsilon = 1e-05
rope_base = 500000.0
LOG2E = 1.4426950408889634
SCALE = HEAD_SIZE ** (-0.5) * LOG2E
FLOOR = -1e29
MASKED = -1e30
CHUNK = 128
QTILE = 128
NEAR = 9
LANES = 128
MESH = pl.DeviceIdType.MESH


def tables(positions):
    half = HEAD_SIZE // 2
    freqs = rope_base ** (-jnp.arange(half, dtype=jnp.float32) * 2.0 / HEAD_SIZE)
    angles = positions.astype(jnp.float32)[:, None] * freqs[None, :]
    cosine = jnp.cos(angles)
    sine = jnp.sin(angles)
    return (
        jnp.concatenate([cosine, cosine], axis=1),
        jnp.concatenate([-sine, sine], axis=1),
    )


def columns_of(n_cp):
    chips = n_cp // 2
    cols = 1
    while cols * cols * 4 <= chips:
        cols *= 2
    return cols


def layer_kernel(
    hid_hbm, gain_ref, wq_hbm, wk_hbm, wv_hbm, wo_hbm, cos_ref, sin_ref, docs_ref, qdoc_ref,
    out_hbm,
    hid, wq, kv, q, normed, docs, recv,
    hid_send, hid_recv, own_sem, w_sem, doc_send, doc_recv, kv_send, kv_recv,
    part_send, part_recv, out_sem,
    *, n_cp, n_tp, longest,
):
    tok, feat = hid_hbm.shape
    width = gain_ref.shape[1]
    q_cols = wq.shape[1]
    kv_cols = kv.shape[1]
    n_kv = kv_cols // (2 * HEAD_SIZE)
    chunks = tok // CHUNK
    n_tiles = tok // QTILE
    cols = columns_of(n_cp)
    rows_z = n_cp // (2 * cols)
    window = min((longest + tok - 2) // tok, n_cp - 1)
    chip_window = (window + 1) // 2
    near = min(NEAR, window + 1)

    me = lax.axis_index("cp")
    rank = lax.axis_index("tp")
    core = lax.rem(me, 2)
    my_x = lax.rem(me // 2, cols)
    my_z = me // (2 * cols)

    def peer_of(by):
        return lax.rem(rank + by, n_tp)

    barrier = pltpu.get_barrier_semaphore()
    for by in range(1, n_tp):
        pl.semaphore_signal(barrier, inc=1, device_id={"tp": peer_of(by)}, device_id_type=MESH)

    def greet(by, carry):
        pl.semaphore_signal(
            barrier, inc=1, device_id={"cp": lax.rem(me + by, n_cp)}, device_id_type=MESH
        )
        return carry

    lax.fori_loop(1, n_cp, greet, 0)

    own_copy = pltpu.make_async_copy(hid_hbm, hid.at[rank], own_sem)
    own_copy.start()
    docs[me] = docs_ref[...]
    wq_copy = pltpu.make_async_copy(wq_hbm, wq, w_sem.at[2])

    def hid_copy(by, t):
        rows = pl.ds(t * CHUNK, CHUNK)
        return pltpu.make_async_remote_copy(
            src_ref=hid_hbm.at[rows],
            dst_ref=hid.at[rank, rows],
            send_sem=hid_send.at[by - 1, t],
            recv_sem=hid_recv.at[n_tp - 1 - by, t],
            device_id={"tp": peer_of(by)},
            device_id_type=MESH,
        )

    def doc_copy(source, target):
        return pltpu.make_async_remote_copy(
            src_ref=docs_ref,
            dst_ref=docs.at[source],
            send_sem=doc_send.at[target],
            recv_sem=doc_recv.at[source],
            device_id={"cp": target},
            device_id_type=MESH,
        )

    last_target = jnp.minimum(me + window, n_cp - 1)

    def doc_start(target, carry):
        doc_copy(me, target).start()
        return carry

    def begin():
        pl.semaphore_wait(barrier, n_cp - 1 + n_tp - 1)
        for t in range(chunks):
            for by in range(1, n_tp):
                hid_copy(by, t).start()
        lax.fori_loop(me + 1, last_target + 1, doc_start, 0)

    def takes(z, x, zs, xs):
        reach = z * cols - (zs * cols + xs) <= chip_window
        by_z = (xs == x) & (zs < z) & reach
        from_left = (xs < x) & (zs <= z) & (z * cols + x - (zs * cols + xs) <= chip_window)
        from_right = (xs > x) & (zs < z) & reach
        return by_z | from_left | from_right

    def block_copy(direction, zs, xs, ks, t, target):
        chip = zs * cols + xs
        s = chip * 2 + ks
        rows = pl.ds(pl.multiple_of(s * tok + t * CHUNK, CHUNK), CHUNK)
        return pltpu.make_async_remote_copy(
            src_ref=kv.at[rows],
            dst_ref=kv.at[rows],
            send_sem=kv_send.at[direction, chip * chunks + t],
            recv_sem=kv_recv.at[s * chunks + t],
            device_id={"cp": target},
            device_id_type=MESH,
        )

    def hops(zs, xs):
        own_chip = (zs == my_z) & (xs == my_x)
        return (
            ((xs == my_x) & (my_z + 1 < rows_z) & takes(my_z + 1, my_x, zs, xs), me + 2 * cols),
            ((xs <= my_x) & (my_x + 1 < cols) & takes(my_z, my_x + 1, zs, xs), me + 2),
            ((xs >= my_x) & (my_x >= 1) & takes(my_z, my_x - 1, zs, xs), me - 2),
            (jnp.logical_not(own_chip) | (core == 0), me + 1 - 2 * core),
        )

    def forward(zs, xs, t):
        for direction, (wanted, target) in enumerate(hops(zs, xs)):
            @pl.when(wanted)
            def _():
                block_copy(direction, zs, xs, core, t, target).start()

    def arrive(zs, xs, ks, t, relay):
        in_range = (zs >= 0) & (xs >= 0) & (xs < cols) & (t >= 0) & (t < chunks)
        own_chip = (zs == my_z) & (xs == my_x)
        if relay:
            wanted = in_range & takes(my_z, my_x, zs, xs)
        else:
            wanted = in_range & (takes(my_z, my_x, zs, xs) | (own_chip & (core == 1)))

        @pl.when(wanted)
        def _():
            block_copy(0, zs, xs, ks, t, me).wait_recv()
            if relay:
                forward(zs, xs, t)

    stages = [[] for _ in range(chunks + (rows_z - 1) * chunks + 3)]
    settled = {0: chunks + 1}
    late = [
        (dz, group + 1 - dz)
        for group in range(chunks - 1, chunks + rows_z - 2)
        for dz in range(1, rows_z)
        if 0 <= group + 1 - dz < chunks
    ]
    for dz in range(rows_z):
        for t in range(chunks):
            if dz == 0:
                first = t
            elif (dz, t) in late:
                first = chunks + late.index((dz, t))
            else:
                first = t + dz - 1
            if dz:
                stages[first].append((0, dz, t))
            stages[first + 1].append((1, dz, t))
            stages[first + 2].append((2, dz, t))
            settled[dz] = max(settled.get(dz, 0), first + 2)
    while not stages[-1]:
        stages.pop()
    for stage_events in stages:
        stage_events.sort()

    def run_stage(k):
        for i, events in enumerate(stages):
            @pl.when(k == i)
            def _():
                for kind, dz, t in events:
                    if kind == 0:
                        arrive(my_z - dz, my_x, core, t, True)
                for dx in range(1, cols):
                    for kind, dz, t in events:
                        if kind == 1:
                            arrive(my_z - dz, my_x - dx, core, t, True)
                            arrive(my_z - dz, my_x + dx, core, t, True)
                for kind, dz, t in events:
                    if kind == 2:
                        def from_core(xs, carry):
                            own_chip = (dz == 0) & (xs == my_x)

                            @pl.when(jnp.logical_not(own_chip))
                            def _():
                                arrive(my_z - dz, xs, 1 - core, t, False)

                            return carry

                        lax.fori_loop(0, cols, from_core, 0)
                if i == chunks - 1:
                    for t in range(chunks):
                        arrive(my_z, my_x, 1 - core, t, False)

    def projections(wkv):
        wk_copy = pltpu.make_async_copy(wk_hbm, wkv.at[:, pl.ds(0, kv_cols // 2)], w_sem.at[0])
        wv_copy = pltpu.make_async_copy(
            wv_hbm, wkv.at[:, pl.ds(kv_cols // 2, kv_cols // 2)], w_sem.at[1]
        )
        wk_copy.start()
        wv_copy.start()
        wq_copy.start()
        begin()
        own_copy.wait()
        wk_copy.wait()
        wv_copy.wait()
        part_rows = 32

        def rope(raw, cosine, sine):
            turned = raw * cosine + pltpu.roll(raw, HEAD_SIZE // 2, 1) * sine
            return turned.astype(jnp.bfloat16)

        def chunk_step(t, carry):
            base = pl.multiple_of(t * CHUNK, CHUNK)
            for by in range(1, n_tp):
                pltpu.make_async_remote_copy(
                    src_ref=hid.at[peer_of(by), pl.ds(base, CHUNK)],
                    dst_ref=hid.at[peer_of(by), pl.ds(base, CHUNK)],
                    send_sem=hid_send.at[by - 1, t],
                    recv_sem=hid_recv.at[by - 1, t],
                    device_id={"tp": peer_of(by)},
                    device_id_type=MESH,
                ).wait_recv()

            def norm_part(i, carry):
                rows = pl.ds(pl.multiple_of(base + i * part_rows, part_rows), part_rows)
                total = jnp.zeros((part_rows, LANES), jnp.float32)
                for j in range(n_tp):
                    wide = hid[j, rows, :].astype(jnp.float32)
                    square = wide * wide
                    for c in range(feat // LANES):
                        total = total + square[:, c * LANES : (c + 1) * LANES]
                mean = jnp.sum(total, axis=1, keepdims=True) / width
                inverse_rms = lax.rsqrt(mean + epsilon)
                out_rows = pl.ds(pl.multiple_of(i * part_rows, part_rows), part_rows)
                for j in range(n_tp):
                    wide = hid[j, rows, :].astype(jnp.float32)
                    gain = gain_ref[:, j * feat : (j + 1) * feat]
                    normed[out_rows, j * feat : (j + 1) * feat] = (
                        wide * inverse_rms * gain
                    ).astype(jnp.bfloat16)
                return carry

            lax.fori_loop(0, CHUNK // part_rows, norm_part, 0)
            rows = pl.ds(base, CHUNK)
            cosine = cos_ref[rows, :]
            sine = sin_ref[rows, :]
            own_rows = pl.ds(pl.multiple_of(me * tok + t * CHUNK, CHUNK), CHUNK)
            for g in range(2 * n_kv):
                lanes = slice(g * HEAD_SIZE, (g + 1) * HEAD_SIZE)
                if g % 2 == 0:
                    pair = jnp.dot(
                        normed[...],
                        wkv[:, g * HEAD_SIZE : (g + 2) * HEAD_SIZE],
                        preferred_element_type=jnp.float32,
                    )
                raw = pair[:, (g % 2) * HEAD_SIZE : (g % 2 + 1) * HEAD_SIZE]
                kv[own_rows, lanes] = rope(raw, cosine, sine) if g < n_kv else raw.astype(jnp.bfloat16)

            @pl.when(t == 0)
            def _():
                wq_copy.wait()

            def query_group(g, carry):
                cut = pl.multiple_of(g * GROUP * HEAD_SIZE, HEAD_SIZE)
                raw = jnp.dot(
                    normed[...],
                    wq[:, pl.ds(cut, GROUP * HEAD_SIZE)],
                    preferred_element_type=jnp.float32,
                )
                for h in range(GROUP):
                    q[g * GROUP + h, rows, :] = rope(
                        raw[:, h * HEAD_SIZE : (h + 1) * HEAD_SIZE], cosine, sine
                    )
                return carry

            query_group(0, 0)
            forward(my_z, my_x, t)
            lax.fori_loop(1, n_kv, query_group, 0)
            run_stage(t)
            return carry

        lax.fori_loop(0, chunks, chunk_step, 0)

    pl.run_scoped(projections, pltpu.VMEM((width, kv_cols), jnp.bfloat16))

    wo_copies = [
        pltpu.make_async_copy(
            wo_hbm.at[:, pl.ds(j * feat, feat)], wq.at[pl.ds(j * q_cols, q_cols)], w_sem.at[3 + j]
        )
        for j in range(n_tp)
    ]
    for copy in wo_copies:
        copy.start()

    def attention(acc, best, denom, stage):
        strips = feat // LANES
        block_lanes = tok // LANES
        def doc_strip(s):
            return s // strips, pl.ds(pl.multiple_of(lax.rem(s, strips) * LANES, LANES), LANES)

        def key_docs(s):
            row = jnp.broadcast_to(docs[s], (LANES, tok))
            number = lax.broadcasted_iota(jnp.int32, (LANES, tok), 0)
            one_hot = jnp.where(row == number, 1.0, 0.0).astype(jnp.float32)
            j, lanes = doc_strip(s)
            hid[j, :, lanes] = one_hot.T.astype(jnp.bfloat16)

        def attend(g, start, size, blocks, first=False):
            count = len(blocks)
            key_rows = pl.ds(pl.multiple_of(blocks[0] * tok, tok), count * tok)
            key_lanes = pl.ds(pl.multiple_of(g * HEAD_SIZE, HEAD_SIZE), HEAD_SIZE)
            value_lanes = pl.ds(pl.multiple_of((n_kv + g) * HEAD_SIZE, HEAD_SIZE), HEAD_SIZE)
            numbers = []
            for s in blocks:
                j, lanes = doc_strip(s)
                numbers.append(hid[j, :, lanes])
            numbers = numbers[0] if count == 1 else jnp.concatenate(numbers, axis=0)
            keys = jnp.concatenate([kv[key_rows, key_lanes], numbers], axis=1)
            rows = pl.ds(start, size)
            heads = pl.ds(g * GROUP, GROUP)
            stacked = GROUP * size
            others = jnp.concatenate([qdoc_ref[rows, :]] * GROUP, axis=0)
            queries = jnp.concatenate(
                [q[heads, rows, :].reshape(stacked, HEAD_SIZE), others], axis=1
            )
            scores = lax.dot_general(
                queries, keys, (((1,), (1,)), ((), ())), preferred_element_type=jnp.float32
            )
            pieces = [
                scores[:, c * LANES : (c + 1) * LANES] * SCALE for c in range(count * block_lanes)
            ]
            if first:
                row = lax.broadcasted_iota(jnp.int32, (stacked, LANES), 0) % size
                lane = lax.broadcasted_iota(jnp.int32, (stacked, LANES), 1)
                pieces = [
                    jnp.where(row >= lane + c * LANES, p, MASKED) for c, p in enumerate(pieces)
                ]
            top = jnp.max(functools.reduce(jnp.maximum, pieces), axis=1, keepdims=True)
            shape = (GROUP, size, LANES)
            if first:
                new = jnp.broadcast_to(jnp.maximum(top, FLOOR), (stacked, LANES))
            else:
                old = best[heads, rows, :].reshape(stacked, LANES)
                new = jnp.maximum(old, top)
                correction = jnp.exp2(old - new)
            weights = [jnp.exp2(p - new) for p in pieces]
            total = functools.reduce(jnp.add, weights)
            rounded = jnp.concatenate([w.astype(jnp.bfloat16) for w in weights], axis=1)
            sums = jnp.dot(rounded, kv[key_rows, value_lanes], preferred_element_type=jnp.float32)
            if not first:
                total = denom[heads, rows, :].reshape(stacked, LANES) * correction + total
                sums = acc[heads, rows, :].reshape(stacked, LANES) * correction + sums
            best[heads, rows, :] = new.reshape(shape)
            denom[heads, rows, :] = total.reshape(shape)
            acc[heads, rows, :] = sums.reshape(shape)

        def all_tiles(s, first):
            def one(g, carry):
                attend(g, 0, tok, [s], first)
                return carry

            lax.fori_loop(0, n_kv, one, 0)

        key_docs(me)
        all_tiles(me, True)

        in_row = lax.rem(me, 2 * cols) + 1
        last_stage = len(stages) - 1

        def stages_before(o):
            distance = jnp.where(o < in_row, 0, (o - in_row) // (2 * cols) + 1)
            needed = jnp.where((o == 1) & (core == 1), chunks - 1, settled[0])
            for dz in range(1, rows_z):
                needed = jnp.where(distance >= dz, settled[dz], needed)
            return jnp.clip(jnp.maximum(chunks - 1 + o, needed), chunks - 1, last_stage)

        def take_stages(begin, end):
            def one(k, carry):
                run_stage(k)
                return carry

            lax.fori_loop(begin, end, one, 0)

        def docs_for(s):
            doc_copy(s, me).wait_recv()
            key_docs(s)

        def near_step(o, carry):
            take_stages(
                jnp.where(o == 1, chunks, stages_before(o - 1) + 1), stages_before(o) + 1
            )
            s = me - o

            @pl.when(s >= 0)
            def _():
                docs_for(s)
                all_tiles(s, False)

            return carry

        lax.fori_loop(1, near, near_step, 0)
        take_stages(stages_before(near - 1) + 1, last_stage + 1)

        def far_docs(o, carry):
            @pl.when(me - o >= 0)
            def _():
                docs_for(me - o)

            return carry

        lax.fori_loop(near, window + 1, far_docs, 0)
        for copy in wo_copies:
            copy.wait()

        n_far = jnp.maximum(jnp.minimum(window, me) + 1 - near, 0)
        col_step = min(512, feat)

        def part_copy(by, tile):
            rows = pl.ds(pl.multiple_of(tile * QTILE, QTILE), QTILE)
            return pltpu.make_async_remote_copy(
                src_ref=stage.at[by - 1, rows],
                dst_ref=recv.at[n_tp - 1 - by, rows],
                send_sem=part_send.at[by - 1, tile],
                recv_sem=part_recv.at[n_tp - 1 - by, tile],
                device_id={"tp": peer_of(by)},
                device_id_type=MESH,
            )

        def tile_step(tile, carry):
            rows = pl.ds(pl.multiple_of(tile * QTILE, QTILE), QTILE)

            start = pl.multiple_of(tile * QTILE, QTILE)

            def far_pair(i, carry):
                s = me - near - 1 - 2 * (i // n_kv)
                attend(lax.rem(i, n_kv), start, QTILE, [s, s + 1])
                return carry

            lax.fori_loop(0, n_far // 2 * n_kv, far_pair, 0)

            def far_last(g, carry):
                attend(g, start, QTILE, [me - near - n_far + 1])
                return carry

            lax.fori_loop(0, lax.rem(n_far, 2) * n_kv, far_last, 0)

            def finish(head, carry):
                total = jnp.sum(denom[head, rows, :], axis=1, keepdims=True)
                lanes = pl.ds(pl.multiple_of(head * HEAD_SIZE, HEAD_SIZE), HEAD_SIZE)
                normed[:, lanes] = (acc[head, rows, :] / total).astype(jnp.bfloat16)
                return carry

            lax.fori_loop(0, n_kv * GROUP, finish, 0)
            attended = normed[:, :q_cols]
            for by in list(range(1, n_tp)) + [0]:
                piece = pl.ds(pl.multiple_of(peer_of(by) * q_cols, q_cols), q_cols)
                for c in range(feat // col_step):
                    part = jnp.dot(
                        attended,
                        wq[piece, c * col_step : (c + 1) * col_step],
                        preferred_element_type=jnp.float32,
                    ).astype(jnp.bfloat16)
                    if by:
                        stage[by - 1, rows, c * col_step : (c + 1) * col_step] = part
                    else:
                        for h in range(col_step // LANES):
                            q[c * (col_step // LANES) + h, rows, :] = part[
                                :, h * LANES : (h + 1) * LANES
                            ]
            for by in range(1, n_tp):
                part_copy(by, tile).start()
            return carry

        lax.fori_loop(0, n_tiles, tile_step, 0)

        def out_copy(tile):
            rows = pl.ds(pl.multiple_of(tile * QTILE, QTILE), QTILE)
            return pltpu.make_async_copy(recv.at[0, rows], out_hbm.at[rows], out_sem.at[tile])

        def sum_step(tile, carry):
            rows = pl.ds(pl.multiple_of(tile * QTILE, QTILE), QTILE)
            for by in range(1, n_tp):
                part_copy(by, tile).wait_recv()
            for c in range(feat // LANES):
                lanes = slice(c * LANES, (c + 1) * LANES)
                total = q[c, rows, :].astype(jnp.float32)
                for by in range(1, n_tp):
                    total = total + recv[by - 1, rows, lanes].astype(jnp.float32)
                recv[0, rows, lanes] = total.astype(jnp.bfloat16)
            out_copy(tile).start()
            return carry

        lax.fori_loop(0, n_tiles, sum_step, 0)

        def end_step(tile, carry):
            for by in range(1, n_tp):
                part_copy(by, tile).wait_send()
            out_copy(tile).wait()
            return carry

        lax.fori_loop(0, n_tiles, end_step, 0)

    state = pltpu.VMEM(q.shape, jnp.float32)
    pl.run_scoped(
        attention, state, state, state, pltpu.VMEM((n_tp - 1, tok, feat), jnp.bfloat16)
    )

    def sent_step(i, carry):
        t = lax.rem(i, chunks)
        chip = i // chunks
        zs, xs = chip // cols, lax.rem(chip, cols)
        own_chip = (zs == my_z) & (xs == my_x)
        held = own_chip | ((zs <= my_z) & takes(my_z, my_x, zs, xs))
        for direction, (wanted, target) in enumerate(hops(zs, xs)):
            @pl.when(held & wanted)
            def _():
                block_copy(direction, zs, xs, core, t, target).wait_send()

        return carry

    lax.fori_loop(0, n_cp // 2 * chunks, sent_step, 0)

    def doc_sent(target, carry):
        doc_copy(me, target).wait_send()
        return carry

    lax.fori_loop(me + 1, last_target + 1, doc_sent, 0)
    for t in range(chunks):
        for by in range(1, n_tp):
            hid_copy(by, t).wait_send()


def shards(hidden, norm_gain, w_query, w_key, w_value, w_out, doc_ids, *, n_cp, n_tp):
    tok, feat = hidden.shape
    width = norm_gain.shape[0]
    q_cols = w_query.shape[1]
    kv_cols = 2 * w_key.shape[1]
    seq = tok * n_cp
    longest = seq * 3 // 4
    chunks = tok // CHUNK
    n_tiles = tok // QTILE
    cp_rank = lax.axis_index("cp")
    positions = cp_rank * tok + jnp.arange(tok, dtype=jnp.int32)
    cosine, sine = tables(positions)
    number = jnp.arange(LANES, dtype=jnp.int32)
    other_docs = jnp.where(doc_ids[:, None] == number[None, :], 0.0, MASKED).astype(jnp.bfloat16)
    vmem = pl.BlockSpec(memory_space=pltpu.VMEM)
    hbm = pl.BlockSpec(memory_space=pl.ANY)
    bf16 = jnp.bfloat16
    dma = pltpu.SemaphoreType.DMA
    heads = q_cols // HEAD_SIZE
    return pl.pallas_call(
        functools.partial(layer_kernel, n_cp=n_cp, n_tp=n_tp, longest=longest),
        out_shape=jax.ShapeDtypeStruct((tok, feat), bf16),
        in_specs=[hbm, vmem, hbm, hbm, hbm, hbm, vmem, vmem, vmem, vmem],
        out_specs=hbm,
        scratch_shapes=[
            pltpu.VMEM((n_tp, tok, feat), bf16),
            pltpu.VMEM((width, q_cols), bf16),
            pltpu.VMEM((seq, kv_cols), bf16),
            pltpu.VMEM((heads, tok, HEAD_SIZE), bf16),
            pltpu.VMEM((CHUNK, width), bf16),
            pltpu.VMEM((n_cp, 1, tok), jnp.int32),
            pltpu.VMEM((n_tp - 1, tok, feat), bf16),
            dma((n_tp - 1, chunks)),
            dma((n_tp - 1, chunks)),
            dma(()),
            dma((3 + n_tp,)),
            dma((n_cp,)),
            dma((n_cp,)),
            dma((4, n_cp // 2 * chunks)),
            dma((n_cp * chunks,)),
            dma((n_tp - 1, n_tiles)),
            dma((n_tp - 1, n_tiles)),
            dma((n_tiles,)),
        ],
        compiler_params=pltpu.CompilerParams(
            collective_id=0, has_side_effects=True, vmem_limit_bytes=67_000_000
        ),
    )(
        hidden, norm_gain[None, :], w_query, w_key, w_value, w_out, cosine, sine,
        doc_ids[None, :], other_docs,
    )


def solution(mesh):
    in_specs = (
        P("cp", "tp"),
        P(),
        P(None, "tp"),
        P(None, "tp"),
        P(None, "tp"),
        P("tp", None),
        P("cp"),
    )
    body = functools.partial(shards, n_cp=mesh.shape["cp"], n_tp=mesh.shape["tp"])
    return jax.shard_map(
        body, mesh=mesh, in_specs=in_specs, out_specs=P("cp", "tp"), check_vma=False
    )
```

time: 501 us -> 218 us (0.44)
  Pallas kernels: 494 us -> 211 us
    pallas_call x1, Pallas kernels: 494 us -> 211 us  [shards(): pl.pallas_call(functools.partial(layer_kernel, n_cp=n_cp, n_tp=n_tp, long...]
where the time goes in v1:
time: 218 us
  Pallas kernels  211 us (97%)
  other arithmetic  3.5 us (2%)
  local copies, waits for them, and re-layouts  3.16 us (1%)
    pallas_call x1, Pallas kernels, shards(): pl.pallas_call(functools.partial(layer_kernel, n_cp=n_cp, n_tp=n_tp, long...  211 us

profile of v1, /device:TPU:28, one launch (start us, length us, event | category | flops | bytes accessed | tf_op | source)
XLA Modules:
  0.0 217.6 jit_solution(9883101711726823094)
XLA Ops:
  0.0 1.5 select_convert_fusion.qdoc_ref
  1.5 1.0 fusion
  2.5 1.0 pad_maximum_fusion
  3.5 210.9 %shard_map.73 = bf16[512,2048]{1,0:T(8,128)(2,1)} custom-call(bf16[512,2048]{1,0:T(8,128)(2,1)} %hid_hbm.1, f32[1,4096]{1,0:T(1,128)} %bitcast.2, bf16[4096,2048]{1,0:T(8,128)(2,1)} %wq_hbm.1, bf16[4096,512]{1,0:T(8,128)(2,1)} %wk_hbm.1, bf16[4096,512]{1,0:T(8,128)(2,1)} %wv_hbm.1, bf16[2048,4096]{1,0:T(8,128)(2,1)} %wo_hbm.1, ...), custom_call_target="tpu_custom_call" | custom-call | tf_op jit(solution)/shard_map/pallas_call | solution.py:590
  214.4 3.2 %copy.9 = bf16[512,2048]{1,0:T(8,128)(2,1)} copy(bf16[512,2048]{1,0:T(8,128)(2,1)} %shard_map.73) | data formatting | bytes 4194304
  (2 shorter events, 0.0 us)

commit v2 on v1

--- a/solution.py
+++ b/solution.py
@@ -20,7 +20,6 @@
 MASKED = -1e30
 CHUNK = 128
 QTILE = 128
-NEAR = 9
 LANES = 128
 MESH = pl.DeviceIdType.MESH
 
@@ -46,15 +45,15 @@
 
 
 def layer_kernel(
-    hid_hbm, gain_ref, wq_hbm, wk_hbm, wv_hbm, wo_hbm, cos_ref, sin_ref, docs_ref, qdoc_ref,
-    out_hbm,
-    hid, wq, kv, q, normed, docs, recv,
-    hid_send, hid_recv, own_sem, w_sem, doc_send, doc_recv, kv_send, kv_recv,
+    hid_hbm, gain_hbm, wq_hbm, wk_hbm, wv_hbm, wo_hbm, cos_ref, sin_ref, docs_hbm,
+    own_hbm, got_hbm,
+    hid, wq, kv, q, normed, docs, qdoc, gain, mine,
+    hid_send, hid_recv, own_sem, small_sem, w_sem, doc_send, doc_recv, kv_send, kv_recv,
     part_send, part_recv, out_sem,
     *, n_cp, n_tp, longest,
 ):
     tok, feat = hid_hbm.shape
-    width = gain_ref.shape[1]
+    width = gain_hbm.shape[0]
     q_cols = wq.shape[1]
     kv_cols = kv.shape[1]
     n_kv = kv_cols // (2 * HEAD_SIZE)
@@ -64,7 +63,8 @@
     rows_z = n_cp // (2 * cols)
     window = min((longest + tok - 2) // tok, n_cp - 1)
     chip_window = (window + 1) // 2
-    near = min(NEAR, window + 1)
+    pairs = (window + 1) // 2
+    half = tok // 2
 
     me = lax.axis_index("cp")
     rank = lax.axis_index("tp")
@@ -89,7 +89,10 @@
 
     own_copy = pltpu.make_async_copy(hid_hbm, hid.at[rank], own_sem)
     own_copy.start()
-    docs[me] = docs_ref[...]
+    gain_copy = pltpu.make_async_copy(gain_hbm, gain.at[0], small_sem.at[0])
+    docs_copy = pltpu.make_async_copy(docs_hbm, docs.at[me, 0], small_sem.at[1])
+    gain_copy.start()
+    docs_copy.start()
     wq_copy = pltpu.make_async_copy(wq_hbm, wq, w_sem.at[2])
 
     def hid_copy(by, t):
@@ -105,7 +108,7 @@
 
     def doc_copy(source, target):
         return pltpu.make_async_remote_copy(
-            src_ref=docs_ref,
+            src_ref=docs.at[source],
             dst_ref=docs.at[source],
             send_sem=doc_send.at[target],
             recv_sem=doc_recv.at[source],
@@ -124,7 +127,9 @@
         for t in range(chunks):
             for by in range(1, n_tp):
                 hid_copy(by, t).start()
+        docs_copy.wait()
         lax.fori_loop(me + 1, last_target + 1, doc_start, 0)
+        gain_copy.wait()
 
     def takes(z, x, zs, xs):
         reach = z * cols - (zs * cols + xs) <= chip_window
@@ -175,31 +180,43 @@
             if relay:
                 forward(zs, xs, t)
 
-    stages = [[] for _ in range(chunks + (rows_z - 1) * chunks + 3)]
-    settled = {0: chunks + 1}
-    late = [
-        (dz, group + 1 - dz)
-        for group in range(chunks - 1, chunks + rows_z - 2)
+    along = {}
+    for dz in range(1, rows_z):
+        for t in range(chunks):
+            group = dz + t - 1
+            if group == 0 or (group < chunks - 1 and (dz > 1 or group < chunks - 2)):
+                along[dz, t] = group
+            elif group == chunks - 2:
+                along[dz, t] = chunks - 1
+    late = sorted(
+        (dz + t, t if t == chunks - 1 and dz == 1 else 0, dz, t)
         for dz in range(1, rows_z)
-        if 0 <= group + 1 - dz < chunks
-    ]
+        for t in range(chunks)
+        if (dz, t) not in along
+    )
+    late = [(dz, t) for _, _, dz, t in late]
+    for i, event in enumerate(late):
+        along[event] = chunks + 1 + 2 * i
+
+    def later(stage, busy, calm):
+        return stage + (calm if stage < chunks - 1 else busy)
+
+    stages = [[] for _ in range(3 * chunks + 2 * len(late) + 16)]
+    settled = {}
     for dz in range(rows_z):
         for t in range(chunks):
-            if dz == 0:
-                first = t
-            elif (dz, t) in late:
-                first = chunks + late.index((dz, t))
-            else:
-                first = t + dz - 1
+            first = along[dz, t] if dz else t
             if dz:
                 stages[first].append((0, dz, t))
-            stages[first + 1].append((1, dz, t))
-            stages[first + 2].append((2, dz, t))
-            settled[dz] = max(settled.get(dz, 0), first + 2)
+            by_x = later(first, 3, 1)
+            stages[by_x].append((1, dz, t))
+            stages[by_x + 1].append((2, dz, t))
+            if t < chunks // 2:
+                settled[dz] = max(settled.get(dz, 0), by_x + 1)
+    for dz in range(1, rows_z):
+        settled[dz] = max(settled[dz], settled[dz - 1])
     while not stages[-1]:
         stages.pop()
-    for stage_events in stages:
-        stage_events.sort()
 
     def run_stage(k):
         for i, events in enumerate(stages):
@@ -245,7 +262,7 @@
 
         def rope(raw, cosine, sine):
             turned = raw * cosine + pltpu.roll(raw, HEAD_SIZE // 2, 1) * sine
-            return turned.astype(jnp.bfloat16)
+            return turned
 
         def chunk_step(t, carry):
             base = pl.multiple_of(t * CHUNK, CHUNK)
@@ -272,9 +289,9 @@
                 out_rows = pl.ds(pl.multiple_of(i * part_rows, part_rows), part_rows)
                 for j in range(n_tp):
                     wide = hid[j, rows, :].astype(jnp.float32)
-                    gain = gain_ref[:, j * feat : (j + 1) * feat]
+                    scale = gain[:, j * feat : (j + 1) * feat]
                     normed[out_rows, j * feat : (j + 1) * feat] = (
-                        wide * inverse_rms * gain
+                        wide * inverse_rms * scale
                     ).astype(jnp.bfloat16)
                 return carry
 
@@ -292,7 +309,8 @@
                         preferred_element_type=jnp.float32,
                     )
                 raw = pair[:, (g % 2) * HEAD_SIZE : (g % 2 + 1) * HEAD_SIZE]
-                kv[own_rows, lanes] = rope(raw, cosine, sine) if g < n_kv else raw.astype(jnp.bfloat16)
+                turned = rope(raw, cosine, sine) if g < n_kv else raw
+                kv[own_rows, lanes] = turned.astype(jnp.bfloat16)
 
             @pl.when(t == 0)
             def _():
@@ -306,9 +324,8 @@
                     preferred_element_type=jnp.float32,
                 )
                 for h in range(GROUP):
-                    q[g * GROUP + h, rows, :] = rope(
-                        raw[:, h * HEAD_SIZE : (h + 1) * HEAD_SIZE], cosine, sine
-                    )
+                    turned = rope(raw[:, h * HEAD_SIZE : (h + 1) * HEAD_SIZE], cosine, sine)
+                    q[g * GROUP + h, rows, :] = (turned * SCALE).astype(jnp.bfloat16)
                 return carry
 
             query_group(0, 0)
@@ -332,32 +349,39 @@
 
     def attention(acc, best, denom, stage):
         strips = feat // LANES
-        block_lanes = tok // LANES
         def doc_strip(s):
             return s // strips, pl.ds(pl.multiple_of(lax.rem(s, strips) * LANES, LANES), LANES)
 
-        def key_docs(s):
+        def docs_columns(s, other, same):
             row = jnp.broadcast_to(docs[s], (LANES, tok))
             number = lax.broadcasted_iota(jnp.int32, (LANES, tok), 0)
-            one_hot = jnp.where(row == number, 1.0, 0.0).astype(jnp.float32)
+            return jnp.where(row == number, same, other).astype(jnp.float32).T.astype(jnp.bfloat16)
+
+        def key_docs(s):
             j, lanes = doc_strip(s)
-            hid[j, :, lanes] = one_hot.T.astype(jnp.bfloat16)
-
-        def attend(g, start, size, blocks, first=False):
-            count = len(blocks)
-            key_rows = pl.ds(pl.multiple_of(blocks[0] * tok, tok), count * tok)
+            hid[j, :, lanes] = docs_columns(s, 0.0, 1.0)
+
+        def attend(g, start, size, segments, first=False):
             key_lanes = pl.ds(pl.multiple_of(g * HEAD_SIZE, HEAD_SIZE), HEAD_SIZE)
             value_lanes = pl.ds(pl.multiple_of((n_kv + g) * HEAD_SIZE, HEAD_SIZE), HEAD_SIZE)
-            numbers = []
-            for s in blocks:
-                j, lanes = doc_strip(s)
-                numbers.append(hid[j, :, lanes])
-            numbers = numbers[0] if count == 1 else jnp.concatenate(numbers, axis=0)
-            keys = jnp.concatenate([kv[key_rows, key_lanes], numbers], axis=1)
+            keys, values = [], []
+            for block, begin, length in segments:
+                present = (block >= 0) & (me - block <= window)
+                block = jnp.where(present, block, me)
+                j, lanes = doc_strip(block)
+                numbers = hid[j, begin : begin + length, lanes]
+                if not first:
+                    numbers = jnp.where(present, numbers, jnp.ones_like(numbers))
+                key_rows = pl.ds(pl.multiple_of(block * tok + begin, length), length)
+                keys.append(jnp.concatenate([kv[key_rows, key_lanes], numbers], axis=1))
+                values.append(kv[key_rows, value_lanes])
+            keys = jnp.concatenate(keys, axis=0)
+            values = jnp.concatenate(values, axis=0)
+            key_count = keys.shape[0]
             rows = pl.ds(start, size)
             heads = pl.ds(g * GROUP, GROUP)
             stacked = GROUP * size
-            others = jnp.concatenate([qdoc_ref[rows, :]] * GROUP, axis=0)
+            others = jnp.concatenate([qdoc[rows, :]] * GROUP, axis=0)
             queries = jnp.concatenate(
                 [q[heads, rows, :].reshape(stacked, HEAD_SIZE), others], axis=1
             )
@@ -365,7 +389,7 @@
                 queries, keys, (((1,), (1,)), ((), ())), preferred_element_type=jnp.float32
             )
             pieces = [
-                scores[:, c * LANES : (c + 1) * LANES] * SCALE for c in range(count * block_lanes)
+                scores[:, c * LANES : (c + 1) * LANES] for c in range(key_count // LANES)
             ]
             if first:
                 row = lax.broadcasted_iota(jnp.int32, (stacked, LANES), 0) % size
@@ -384,7 +408,7 @@
             weights = [jnp.exp2(p - new) for p in pieces]
             total = functools.reduce(jnp.add, weights)
             rounded = jnp.concatenate([w.astype(jnp.bfloat16) for w in weights], axis=1)
-            sums = jnp.dot(rounded, kv[key_rows, value_lanes], preferred_element_type=jnp.float32)
+            sums = jnp.dot(rounded, values, preferred_element_type=jnp.float32)
             if not first:
                 total = denom[heads, rows, :].reshape(stacked, LANES) * correction + total
                 sums = acc[heads, rows, :].reshape(stacked, LANES) * correction + sums
@@ -392,25 +416,24 @@
             denom[heads, rows, :] = total.reshape(shape)
             acc[heads, rows, :] = sums.reshape(shape)
 
-        def all_tiles(s, first):
+        def groups(begin, end, segments, first=False):
             def one(g, carry):
-                attend(g, 0, tok, [s], first)
+                attend(g, 0, tok, segments, first)
                 return carry
 
-            lax.fori_loop(0, n_kv, one, 0)
-
-        key_docs(me)
-        all_tiles(me, True)
+            lax.fori_loop(begin, end, one, 0)
+
 
         in_row = lax.rem(me, 2 * cols) + 1
         last_stage = len(stages) - 1
 
-        def stages_before(o):
+        def stages_by(p):
+            o = 2 * (p // 2)
             distance = jnp.where(o < in_row, 0, (o - in_row) // (2 * cols) + 1)
-            needed = jnp.where((o == 1) & (core == 1), chunks - 1, settled[0])
+            needed = jnp.where(o == 0, 0, settled[0])
             for dz in range(1, rows_z):
-                needed = jnp.where(distance >= dz, settled[dz], needed)
-            return jnp.clip(jnp.maximum(chunks - 1 + o, needed), chunks - 1, last_stage)
+                needed = jnp.where((distance >= dz) & (o > 0), settled[dz], needed)
+            return jnp.clip(jnp.maximum(chunks - 1 + p, needed), chunks - 1, last_stage)
 
         def take_stages(begin, end):
             def one(k, carry):
@@ -423,64 +446,73 @@
             doc_copy(s, me).wait_recv()
             key_docs(s)
 
-        def near_step(o, carry):
-            take_stages(
-                jnp.where(o == 1, chunks, stages_before(o - 1) + 1), stages_before(o) + 1
-            )
-            s = me - o
-
-            @pl.when(s >= 0)
-            def _():
-                docs_for(s)
-                all_tiles(s, False)
+        key_docs(me)
+        own_docs = docs_columns(me, MASKED, 0.0)
+        qdoc[...] = own_docs
+        groups(0, n_kv // 2, [(me, 0, tok)], True)
+        take_stages(chunks, stages_by(1) + 1)
+        groups(n_kv // 2, n_kv, [(me, 0, tok)], True)
+
+        def near_step(i, carry):
+            take_stages(stages_by(2 * i - 1) + 1, stages_by(2 * i) + 1)
+            last = me - 2 * i
+            segments = [(last, 0, half), (last + 1, 0, half)]
+
+            @pl.when(last + 1 >= 0)
+            def _():
+                docs_for(last + 1)
+
+            @pl.when((last >= 0) & (2 * i <= window))
+            def _():
+                docs_for(last)
+
+            @pl.when(last + 1 >= 0)
+            def _():
+                groups(0, n_kv // 2, segments)
+
+            take_stages(stages_by(2 * i) + 1, stages_by(2 * i + 1) + 1)
+
+            @pl.when(last + 1 >= 0)
+            def _():
+                groups(n_kv // 2, n_kv, segments)
 
             return carry
 
-        lax.fori_loop(1, near, near_step, 0)
-        take_stages(stages_before(near - 1) + 1, last_stage + 1)
-
-        def far_docs(o, carry):
-            @pl.when(me - o >= 0)
-            def _():
-                docs_for(me - o)
-
-            return carry
-
-        lax.fori_loop(near, window + 1, far_docs, 0)
+        lax.fori_loop(1, pairs + 1, near_step, 0)
+        take_stages(stages_by(2 * pairs + 1) + 1, last_stage + 1)
         for copy in wo_copies:
             copy.wait()
 
-        n_far = jnp.maximum(jnp.minimum(window, me) + 1 - near, 0)
+        n_far = (jnp.minimum(window, me) + 3) // 4
         col_step = min(512, feat)
 
         def part_copy(by, tile):
             rows = pl.ds(pl.multiple_of(tile * QTILE, QTILE), QTILE)
             return pltpu.make_async_remote_copy(
                 src_ref=stage.at[by - 1, rows],
-                dst_ref=recv.at[n_tp - 1 - by, rows],
+                dst_ref=got_hbm.at[n_tp - 1 - by, rows],
                 send_sem=part_send.at[by - 1, tile],
                 recv_sem=part_recv.at[n_tp - 1 - by, tile],
                 device_id={"tp": peer_of(by)},
                 device_id_type=MESH,
             )
 
+        def mine_copy(tile):
+            rows = pl.ds(pl.multiple_of(tile * QTILE, QTILE), QTILE)
+            return pltpu.make_async_copy(mine.at[rows], own_hbm.at[rows], out_sem.at[tile])
+
         def tile_step(tile, carry):
             rows = pl.ds(pl.multiple_of(tile * QTILE, QTILE), QTILE)
 
             start = pl.multiple_of(tile * QTILE, QTILE)
 
-            def far_pair(i, carry):
-                s = me - near - 1 - 2 * (i // n_kv)
-                attend(lax.rem(i, n_kv), start, QTILE, [s, s + 1])
+            def far_step(i, carry):
+                last = me - 4 * (i // n_kv) - 4
+                segments = [(last + n, half, half) for n in range(4)]
+                attend(lax.rem(i, n_kv), start, QTILE, segments)
                 return carry
 
-            lax.fori_loop(0, n_far // 2 * n_kv, far_pair, 0)
-
-            def far_last(g, carry):
-                attend(g, start, QTILE, [me - near - n_far + 1])
-                return carry
-
-            lax.fori_loop(0, lax.rem(n_far, 2) * n_kv, far_last, 0)
+            lax.fori_loop(0, n_far * n_kv, far_step, 0)
 
             def finish(head, carry):
                 total = jnp.sum(denom[head, rows, :], axis=1, keepdims=True)
@@ -492,48 +524,24 @@
             attended = normed[:, :q_cols]
             for by in list(range(1, n_tp)) + [0]:
                 piece = pl.ds(pl.multiple_of(peer_of(by) * q_cols, q_cols), q_cols)
+                target = stage.at[by - 1] if by else mine
                 for c in range(feat // col_step):
-                    part = jnp.dot(
-                        attended,
-                        wq[piece, c * col_step : (c + 1) * col_step],
-                        preferred_element_type=jnp.float32,
+                    cut = slice(c * col_step, (c + 1) * col_step)
+                    target[rows, cut] = jnp.dot(
+                        attended, wq[piece, cut], preferred_element_type=jnp.float32
                     ).astype(jnp.bfloat16)
-                    if by:
-                        stage[by - 1, rows, c * col_step : (c + 1) * col_step] = part
-                    else:
-                        for h in range(col_step // LANES):
-                            q[c * (col_step // LANES) + h, rows, :] = part[
-                                :, h * LANES : (h + 1) * LANES
-                            ]
-            for by in range(1, n_tp):
-                part_copy(by, tile).start()
+                    if c == 0 and by != 1 % n_tp:
+                        part_copy((by or n_tp) - 1, tile).start()
+            mine_copy(tile).start()
             return carry
 
         lax.fori_loop(0, n_tiles, tile_step, 0)
 
-        def out_copy(tile):
-            rows = pl.ds(pl.multiple_of(tile * QTILE, QTILE), QTILE)
-            return pltpu.make_async_copy(recv.at[0, rows], out_hbm.at[rows], out_sem.at[tile])
-
-        def sum_step(tile, carry):
-            rows = pl.ds(pl.multiple_of(tile * QTILE, QTILE), QTILE)
+        def end_step(tile, carry):
             for by in range(1, n_tp):
                 part_copy(by, tile).wait_recv()
-            for c in range(feat // LANES):
-                lanes = slice(c * LANES, (c + 1) * LANES)
-                total = q[c, rows, :].astype(jnp.float32)
-                for by in range(1, n_tp):
-                    total = total + recv[by - 1, rows, lanes].astype(jnp.float32)
-                recv[0, rows, lanes] = total.astype(jnp.bfloat16)
-            out_copy(tile).start()
-            return carry
-
-        lax.fori_loop(0, n_tiles, sum_step, 0)
-
-        def end_step(tile, carry):
-            for by in range(1, n_tp):
                 part_copy(by, tile).wait_send()
-            out_copy(tile).wait()
+            mine_copy(tile).wait()
             return carry
 
         lax.fori_loop(0, n_tiles, end_step, 0)
@@ -580,18 +588,19 @@
     cp_rank = lax.axis_index("cp")
     positions = cp_rank * tok + jnp.arange(tok, dtype=jnp.int32)
     cosine, sine = tables(positions)
-    number = jnp.arange(LANES, dtype=jnp.int32)
-    other_docs = jnp.where(doc_ids[:, None] == number[None, :], 0.0, MASKED).astype(jnp.bfloat16)
     vmem = pl.BlockSpec(memory_space=pltpu.VMEM)
     hbm = pl.BlockSpec(memory_space=pl.ANY)
     bf16 = jnp.bfloat16
     dma = pltpu.SemaphoreType.DMA
     heads = q_cols // HEAD_SIZE
-    return pl.pallas_call(
+    own, got = pl.pallas_call(
         functools.partial(layer_kernel, n_cp=n_cp, n_tp=n_tp, longest=longest),
-        out_shape=jax.ShapeDtypeStruct((tok, feat), bf16),
-        in_specs=[hbm, vmem, hbm, hbm, hbm, hbm, vmem, vmem, vmem, vmem],
-        out_specs=hbm,
+        out_shape=(
+            jax.ShapeDtypeStruct((tok, feat), bf16),
+            jax.ShapeDtypeStruct((n_tp - 1, tok, feat), bf16),
+        ),
+        in_specs=[hbm] * 6 + [vmem, vmem, hbm],
+        out_specs=(hbm, hbm),
         scratch_shapes=[
             pltpu.VMEM((n_tp, tok, feat), bf16),
             pltpu.VMEM((width, q_cols), bf16),
@@ -599,10 +608,13 @@
             pltpu.VMEM((heads, tok, HEAD_SIZE), bf16),
             pltpu.VMEM((CHUNK, width), bf16),
             pltpu.VMEM((n_cp, 1, tok), jnp.int32),
-            pltpu.VMEM((n_tp - 1, tok, feat), bf16),
+            pltpu.VMEM((tok, LANES), bf16),
+            pltpu.VMEM((1, width), jnp.float32),
+            pltpu.VMEM((tok, feat), bf16),
             dma((n_tp - 1, chunks)),
             dma((n_tp - 1, chunks)),
             dma(()),
+            dma((2,)),
             dma((3 + n_tp,)),
             dma((n_cp,)),
             dma((n_cp,)),
@@ -616,9 +628,12 @@
             collective_id=0, has_side_effects=True, vmem_limit_bytes=67_000_000
         ),
     )(
-        hidden, norm_gain[None, :], w_query, w_key, w_value, w_out, cosine, sine,
-        doc_ids[None, :], other_docs,
+        hidden, norm_gain, w_query, w_key, w_value, w_out, cosine, sine, doc_ids,
     )
+    total = own.astype(jnp.float32)
+    for i in range(n_tp - 1):
+        total = total + got[i].astype(jnp.float32)
+    return total.astype(bf16)
 
 
 def solution(mesh):

time: 218 us -> 201 us (0.922)
  Pallas kernels: 211 us -> 194 us
  local copies, waits for them, and re-layouts: 3.16 us -> 0 us
  other arithmetic: 3.5 us -> 6.43 us
    pallas_call x1, Pallas kernels: 211 us -> 194 us  [shards(): pl.pallas_call(functools.partial(layer_kernel, n_cp=n_cp, n_tp=n_tp, long...]
    unnamed x1 -> x0, local copies, waits for them, and re-layouts: 3.16 us -> none
    convert_element_type x1, other arithmetic: 1.47 us -> 4.44 us  [shards(): return total.astype(bf16)]
where the time goes in v2:
time: 201 us; the launch traced here: 200 us
  Pallas kernels  194 us (97%)
  other arithmetic  6.43 us (3%)
    pallas_call x1, Pallas kernels, shards(): pl.pallas_call(functools.partial(layer_kernel, n_cp=n_cp, n_tp=n_tp, long...  194 us
    convert_element_type x1, other arithmetic, shards(): return total.astype(bf16)  4.44 us

profile of v2, /device:TPU:28, one launch (start us, length us, event | category | flops | bytes accessed | tf_op | source)
XLA Modules:
  0.0 200.4 jit_solution(11066476260383370588)
XLA Ops:
  0.0 1.0 fusion.1
  1.0 1.0 pad_maximum_fusion
  2.0 193.9 %shard_map.73 = (bf16[512,2048]{1,0:T(8,128)(2,1)}, bf16[1,512,2048]{2,1,0:T(8,128)(2,1)}) custom-call(bf16[512,2048]{1,0:T(8,128)(2,1)} %hid_hbm.1, f32[4096]{0:T(1024)} %gain_hbm.1, bf16[4096,2048]{1,0:T(8,128)(2,1)} %wq_hbm.1, bf16[4096,512]{1,0:T(8,128)(2,1)} %wk_hbm.1, bf16[4096,512]{1,0:T(8,128)(2,1)} %wv_hbm.1, bf16[2048,4096]{1,0:T(8,128)(2,1)} %wo_hbm.1, ...), custom_call_target="tpu_custom_call" | custom-call | tf_op jit(solution)/shard_map/pallas_call | solution.py:596
  196.0 4.4 %fusion = bf16[512,2048]{1,0:T(8,128)(2,1)} fusion(bf16[512,2048]{1,0:T(8,128)(2,1)} %get-tuple-element.7, bf16[1,512,2048]{2,1,0:T(8,128)(2,1)} %get-tuple-element.8), kind=kLoop, calls=%fused_computation.1 | loop fusion | flops 4194304 | bytes 6291456 | tf_op jit(solution)/shard_map/convert_element_type | solution.py:636
  (2 shorter events, 0.0 us)
